TPU v7x, 128 devices: a whole 4x4x4 slice. The times are simulated.
128 devices in a mesh: seq: 16 (over z, x_hi, core), tp: 8 (over x_lo, y).
Axes of the slice: x: 4 (x_hi: 2, x_lo: 2; x = x_hi * 2 + x_lo), y: 4, z: 4, core: 2. Of those that a mesh axis runs over, the one named last changes fastest.
Arguments:
- tokens: bfloat16 [2, 3072, 4096], P(None, 'seq', 'tp'), may hold values from -6 to 6
- gate_weight: bfloat16 [4096, 4096], P(None, 'tp'), may hold values from -0.09375 to 0.09375
- cand_weight: bfloat16 [4096, 4096], P(None, 'tp'), may hold values from -0.09375 to 0.09375
- forget_bias: float32 [4096], P('tp'), may hold values from -1 to 9
- readout: bfloat16 [2, 3072, 4096], P(None, 'seq', 'tp'), may hold values from -6 to 6
- advantage: int32 [2, 3072], P(None, 'seq'), may hold values from -4 to 4
Outputs:
- grad_gate: float32 [4096, 4096], P('seq', 'tp')
- grad_cand: float32 [4096, 4096], P('seq', 'tp')
- grad_tokens: bfloat16 [2, 3072, 4096], P(None, 'seq', 'tp')
All inputs are finite; a program needn't handle non-finite values.
Results may differ from a plain program's by a relative error of at most 0.014.
Values may be sent and summed in bfloat16 or wider, within the bound.
No kernel may reach another device: no remote copies, remote signals or barrier semaphores. Data moves between devices by JAX's collectives and lax.ppermute only.
A program may use at most 128 MiB of HBM per device.

v0:
```python
import jax
import jax.numpy as jnp
from jax import lax
from jax.sharding import PartitionSpec as P


def from_behind(block, axis, distance):
    devices = range(lax.axis_size(axis))
    route = [(i - distance, i) for i in devices if i - distance in devices]
    return lax.ppermute(block, axis, route)


def compose(earlier, later):
    return (earlier[0] * later[0], later[0] * earlier[1] + later[1])


def shards(tokens, gate_weight, cand_weight, forget_bias, readout, advantage):
    whole = lax.all_gather(tokens, "tp", axis=2, tiled=True)
    count = whole.shape[1]
    width = gate_weight.shape[1]
    flat = whole.reshape(-1, whole.shape[2])
    pre = jnp.dot(flat, gate_weight, preferred_element_type=jnp.float32).reshape(2, count, width)
    cand = jnp.dot(flat, cand_weight, preferred_element_type=jnp.float32).reshape(2, count, width)
    keep = jax.nn.sigmoid(pre + forget_bias)
    prod_keep, local_state = lax.associative_scan(compose, (keep, (1.0 - keep) * cand), axis=1)
    span_mul = prod_keep[:, -1]
    span_add = local_state[:, -1]
    devices = lax.axis_size("seq")

    def forward_link(step, incoming):
        return from_behind(span_mul * incoming + span_add, "seq", 1)

    state_in = lax.fori_loop(0, devices - 1, forward_link, jnp.zeros_like(span_add))
    state = local_state + prod_keep * state_in[:, None]
    prev = jnp.concatenate([state_in[:, None], state[:, :-1]], axis=1)
    score = (advantage.astype(jnp.float32) * 0.25)[:, :, None] * readout.astype(jnp.float32)
    coef = jnp.concatenate([keep[:, 1:], jnp.ones_like(keep[:, :1])], axis=1)
    reach, local_adj = lax.associative_scan(compose, (coef, score), reverse=True, axis=1)
    back_mul = keep[:, 0] * reach[:, 0]
    back_add = keep[:, 0] * local_adj[:, 0]

    def backward_link(step, incoming):
        return from_behind(back_mul * incoming + back_add, "seq", -1)

    adjoint_in = lax.fori_loop(0, devices - 1, backward_link, jnp.zeros_like(back_add))
    adjoint = local_adj + reach * adjoint_in[:, None]
    dpre = (adjoint * (prev - cand) * keep * (1.0 - keep)).astype(jnp.bfloat16).reshape(-1, width)
    dcand = (adjoint * (1.0 - keep)).astype(jnp.bfloat16).reshape(-1, width)
    deltas = jnp.concatenate([dpre, dcand], axis=1)
    both = lax.psum_scatter(
        lax.dot_general(
            flat, deltas, (((0,), (0,)), ((), ())), preferred_element_type=jnp.float32
        ).astype(jnp.bfloat16),
        "seq",
        scatter_dimension=0,
        tiled=True,
    ).astype(jnp.float32)
    grad_gate = both[:, :width]
    grad_cand = both[:, width:]
    contract = (((1,), (1,)), ((), ()))
    term = lax.dot_general(dpre, gate_weight, contract, preferred_element_type=jnp.float32)
    term = term + lax.dot_general(dcand, cand_weight, contract, preferred_element_type=jnp.float32)
    term = term.reshape(2, count, flat.shape[1])
    grad_tokens = lax.psum_scatter(term, "tp", scatter_dimension=2, tiled=True).astype(jnp.bfloat16)
    return (grad_gate, grad_cand, grad_tokens)


def solution(mesh):
    in_specs = (
        P(None, "seq", "tp"),
        P(None, "tp"),
        P(None, "tp"),
        P("tp"),
        P(None, "seq", "tp"),
        P(None, "seq"),
    )
    out_specs = (P("seq", "tp"), P("seq", "tp"), P(None, "seq", "tp"))
    return jax.shard_map(shards, mesh=mesh, in_specs=in_specs, out_specs=out_specs, check_vma=False)
```

profile of v0, /device:TPU:1, one launch (start us, length us, event | category | flops | bytes accessed | tf_op | source)
XLA Modules:
  0.0 573.9 jit_solution(16142009129855514117)
XLA Ops:
  11.2 43.2 %all-gather.2.cloned.1.call-done = bf16[2,192,4096]{2,1,0:T(8,128)(2,1)} async-done(((bf16[2,192,512]{2,1,0:T(8,128)(2,1)}), bf16[2,192,4096]{2,1,0:T(8,128)(2,1)}) %all-gather.2.cloned.1.call-update) | async-done | bytes 3145744 | tf_op jit(solution)/shard_map/all_gather | solution.py:18
  157.4 103.2 %while.21 = (s32[]{:T(128)}, f32[2,512]{1,0:T(2,128)S(1)}, f32[2,512]{1,0:T(2,128)S(1)}, f32[2,512]{1,0:T(2,128)S(1)}, s32[]{:T(128)}) while((s32[]{:T(128)}, f32[2,512]{1,0:T(2,128)S(1)}, f32[2,512]{1,0:T(2,128)S(1)}, f32[2,512]{1,0:T(2,128)S(1)}, s32[]{:T(128)}) %tuple.96), condition=%wide.region_3.0_spmd, body=%wide.region_2.0_spmd.sunk | while | flops 2050 | bytes 32869 | solution.py:33
  157.5 7.3 %collective-permute-start.1 = (f32[2,512]{1,0:T(2,128)S(1)}, f32[2,512]{1,0:T(2,128)S(1)}, u32[]{:S(2)}, u32[]{:S(2)}) collective-permute-start(f32[2,512]{1,0:T(2,128)S(1)} %multiply_add_fusion.19), channel_id=1, source_target_pairs={{0,8},{8,16},{16,24},{24,32},{32,40},{40,48},{48,56},{56,64},{64,7... | collective-permute-start | bytes 12296 | tf_op jit(solution)/shard_map/while/body/eval_jaxpr/ppermute | solution.py:10
  165.5 5.7 collective-permute-start.1
  171.9 5.7 collective-permute-start.1
  178.3 5.7 collective-permute-start.1
  184.7 5.7 collective-permute-start.1
  191.2 5.7 collective-permute-start.1
  197.6 5.7 collective-permute-start.1
  204.0 5.7 collective-permute-start.1
  210.4 5.7 collective-permute-start.1
  216.9 6.4 %collective-permute-start.1 = (f32[2,512]{1,0:T(2,128)S(1)}, f32[2,512]{1,0:T(2,128)S(1)}, u32[]{:S(2)}, u32[]{:S(2)}) collective-permute-start(f32[2,512]{1,0:T(2,128)S(1)} %multiply_add_fusion.19), channel_id=1, source_target_pairs={{0,8},{8,16},{16,24},{24,32},{32,40},{40,48},{48,56},{56,64},{64,7... | collective-permute-start | bytes 12296 | tf_op jit(solution)/shard_map/while/body/eval_jaxpr/ppermute | solution.py:10
  224.0 6.6 %collective-permute-start.1 = (f32[2,512]{1,0:T(2,128)S(1)}, f32[2,512]{1,0:T(2,128)S(1)}, u32[]{:S(2)}, u32[]{:S(2)}) collective-permute-start(f32[2,512]{1,0:T(2,128)S(1)} %multiply_add_fusion.19), channel_id=1, source_target_pairs={{0,8},{8,16},{16,24},{24,32},{32,40},{40,48},{48,56},{56,64},{64,7... | collective-permute-start | bytes 12296 | tf_op jit(solution)/shard_map/while/body/eval_jaxpr/ppermute | solution.py:10
  231.4 6.6 %collective-permute-start.1 = (f32[2,512]{1,0:T(2,128)S(1)}, f32[2,512]{1,0:T(2,128)S(1)}, u32[]{:S(2)}, u32[]{:S(2)}) collective-permute-start(f32[2,512]{1,0:T(2,128)S(1)} %multiply_add_fusion.19), channel_id=1, source_target_pairs={{0,8},{8,16},{16,24},{24,32},{32,40},{40,48},{48,56},{56,64},{64,7... | collective-permute-start | bytes 12296 | tf_op jit(solution)/shard_map/while/body/eval_jaxpr/ppermute | solution.py:10
  238.7 6.6 %collective-permute-start.1 = (f32[2,512]{1,0:T(2,128)S(1)}, f32[2,512]{1,0:T(2,128)S(1)}, u32[]{:S(2)}, u32[]{:S(2)}) collective-permute-start(f32[2,512]{1,0:T(2,128)S(1)} %multiply_add_fusion.19), channel_id=1, source_target_pairs={{0,8},{8,16},{16,24},{24,32},{32,40},{40,48},{48,56},{56,64},{64,7... | collective-permute-start | bytes 12296 | tf_op jit(solution)/shard_map/while/body/eval_jaxpr/ppermute | solution.py:10
  246.0 6.6 %collective-permute-start.1 = (f32[2,512]{1,0:T(2,128)S(1)}, f32[2,512]{1,0:T(2,128)S(1)}, u32[]{:S(2)}, u32[]{:S(2)}) collective-permute-start(f32[2,512]{1,0:T(2,128)S(1)} %multiply_add_fusion.19), channel_id=1, source_target_pairs={{0,8},{8,16},{16,24},{24,32},{32,40},{40,48},{48,56},{56,64},{64,7... | collective-permute-start | bytes 12296 | tf_op jit(solution)/shard_map/while/body/eval_jaxpr/ppermute | solution.py:10
  253.3 6.6 %collective-permute-start.1 = (f32[2,512]{1,0:T(2,128)S(1)}, f32[2,512]{1,0:T(2,128)S(1)}, u32[]{:S(2)}, u32[]{:S(2)}) collective-permute-start(f32[2,512]{1,0:T(2,128)S(1)} %multiply_add_fusion.19), channel_id=1, source_target_pairs={{0,8},{8,16},{16,24},{24,32},{32,40},{40,48},{48,56},{56,64},{64,7... | collective-permute-start | bytes 12296 | tf_op jit(solution)/shard_map/while/body/eval_jaxpr/ppermute | solution.py:10
  263.3 110.8 %while.20 = (s32[]{:T(128)}, f32[2,512]{1,0:T(2,128)S(1)}, f32[2,512]{1,0:T(2,128)S(1)}, f32[2,512]{1,0:T(2,128)S(1)}, s32[]{:T(128)}) while((s32[]{:T(128)}, f32[2,512]{1,0:T(2,128)S(1)}, f32[2,512]{1,0:T(2,128)S(1)}, f32[2,512]{1,0:T(2,128)S(1)}, s32[]{:T(128)}) %tuple.94), condition=%wide.region_1.0_spmd, body=%wide.region_0.0_spmd.sunk | while | flops 2050 | bytes 32869 | solution.py:45
  265.2 5.9 %collective-permute-done = f32[2,512]{1,0:T(2,128)S(1)} collective-permute-done((f32[2,512]{1,0:T(2,128)S(1)}, f32[2,512]{1,0:T(2,128)S(1)}, u32[]{:S(2)}, u32[]{:S(2)}) %collective-permute-start) | collective-permute-done | bytes 4128 | tf_op jit(solution)/shard_map/while/body/eval_jaxpr/ppermute | solution.py:10
  280.3 5.9 %collective-permute-done = f32[2,512]{1,0:T(2,128)S(1)} collective-permute-done((f32[2,512]{1,0:T(2,128)S(1)}, f32[2,512]{1,0:T(2,128)S(1)}, u32[]{:S(2)}, u32[]{:S(2)}) %collective-permute-start) | collective-permute-done | bytes 4128 | tf_op jit(solution)/shard_map/while/body/eval_jaxpr/ppermute | solution.py:10
  310.1 5.4 collective-permute-done
  376.7 6.9 %convert_bitcast_fusion = bf16[4096,1024]{0,1:T(8,128)(2,1)} fusion(bf16[384,4096]{1,0:T(8,128)(2,1)S(1)} %bitcast.52, bf16[384,512]{1,0:T(8,128)(2,1)S(1)} %bitcast.44, bf16[384,512]{1,0:T(8,128)(2,1)S(1)} %bitcast.46), kind=kOutput, calls=%fused_computation.2 | convolution fusion | flops 3226992640 | bytes 12320768 | tf_op jit(solution)/shard_map/dot_general | solution.py:51
  392.6 97.4 %reduce-scatter.3.cloned.1.call-done = bf16[256,1024]{0,1:T(8,128)(2,1)} async-done(((bf16[4096,1024]{0,1:T(8,128)(2,1)}), bf16[256,1024]{0,1:T(8,128)(2,1)}) %reduce-scatter.3.cloned.1.call-update) | async-done | bytes 524304 | tf_op jit(solution)/shard_map/reduce_scatter | solution.py:50
  493.1 72.3 %reduce-scatter.5.cloned.1.call-done = f32[2,192,512]{2,1,0:T(8,128)} async-done(((f32[2,192,4096]{2,1,0:T(8,128)}), f32[2,192,512]{2,1,0:T(8,128)}) %reduce-scatter.5.cloned.1.call-update) | async-done | bytes 786448 | tf_op jit(solution)/shard_map/reduce_scatter | solution.py:64
  (372 shorter events, 229.4 us)
Async XLA Ops:
  7.2 47.3 %all-gather.2.cloned.1.call-start = ((), (), s32[]{:S(2)}) async-start(), calls=%async_computation.2 | async-start | bytes 3538944 | tf_op jit(solution)/shard_map/all_gather | solution.py:18
  7.9 482.1 %reduce-scatter.3.cloned.1.call-start = ((), (), s32[]{:S(2)}) async-start(), calls=%async_computation.3 | async-start | bytes 8912896 | tf_op jit(solution)/shard_map/reduce_scatter | solution.py:50
  157.5 8.0 %collective-permute-start.1 = (f32[2,512]{1,0:T(2,128)S(1)}, f32[2,512]{1,0:T(2,128)S(1)}, u32[]{:S(2)}, u32[]{:S(2)}) collective-permute-start(f32[2,512]{1,0:T(2,128)S(1)} %multiply_add_fusion.19), channel_id=1, source_target_pairs={{0,8},{8,16},{16,24},{24,32},{32,40},{40,48},{48,56},{56,64},{64,7... | collective-permute-start | bytes 12296 | tf_op jit(solution)/shard_map/while/body/eval_jaxpr/ppermute | solution.py:10
  216.9 7.2 %collective-permute-start.1 = (f32[2,512]{1,0:T(2,128)S(1)}, f32[2,512]{1,0:T(2,128)S(1)}, u32[]{:S(2)}, u32[]{:S(2)}) collective-permute-start(f32[2,512]{1,0:T(2,128)S(1)} %multiply_add_fusion.19), channel_id=1, source_target_pairs={{0,8},{8,16},{16,24},{24,32},{32,40},{40,48},{48,56},{56,64},{64,7... | collective-permute-start | bytes 12296 | tf_op jit(solution)/shard_map/while/body/eval_jaxpr/ppermute | solution.py:10
  224.0 7.3 %collective-permute-start.1 = (f32[2,512]{1,0:T(2,128)S(1)}, f32[2,512]{1,0:T(2,128)S(1)}, u32[]{:S(2)}, u32[]{:S(2)}) collective-permute-start(f32[2,512]{1,0:T(2,128)S(1)} %multiply_add_fusion.19), channel_id=1, source_target_pairs={{0,8},{8,16},{16,24},{24,32},{32,40},{40,48},{48,56},{56,64},{64,7... | collective-permute-start | bytes 12296 | tf_op jit(solution)/shard_map/while/body/eval_jaxpr/ppermute | solution.py:10
  231.4 7.3 %collective-permute-start.1 = (f32[2,512]{1,0:T(2,128)S(1)}, f32[2,512]{1,0:T(2,128)S(1)}, u32[]{:S(2)}, u32[]{:S(2)}) collective-permute-start(f32[2,512]{1,0:T(2,128)S(1)} %multiply_add_fusion.19), channel_id=1, source_target_pairs={{0,8},{8,16},{16,24},{24,32},{32,40},{40,48},{48,56},{56,64},{64,7... | collective-permute-start | bytes 12296 | tf_op jit(solution)/shard_map/while/body/eval_jaxpr/ppermute | solution.py:10
  238.7 7.3 %collective-permute-start.1 = (f32[2,512]{1,0:T(2,128)S(1)}, f32[2,512]{1,0:T(2,128)S(1)}, u32[]{:S(2)}, u32[]{:S(2)}) collective-permute-start(f32[2,512]{1,0:T(2,128)S(1)} %multiply_add_fusion.19), channel_id=1, source_target_pairs={{0,8},{8,16},{16,24},{24,32},{32,40},{40,48},{48,56},{56,64},{64,7... | collective-permute-start | bytes 12296 | tf_op jit(solution)/shard_map/while/body/eval_jaxpr/ppermute | solution.py:10
  246.0 7.3 %collective-permute-start.1 = (f32[2,512]{1,0:T(2,128)S(1)}, f32[2,512]{1,0:T(2,128)S(1)}, u32[]{:S(2)}, u32[]{:S(2)}) collective-permute-start(f32[2,512]{1,0:T(2,128)S(1)} %multiply_add_fusion.19), channel_id=1, source_target_pairs={{0,8},{8,16},{16,24},{24,32},{32,40},{40,48},{48,56},{56,64},{64,7... | collective-permute-start | bytes 12296 | tf_op jit(solution)/shard_map/while/body/eval_jaxpr/ppermute | solution.py:10
  253.3 7.3 %collective-permute-start.1 = (f32[2,512]{1,0:T(2,128)S(1)}, f32[2,512]{1,0:T(2,128)S(1)}, u32[]{:S(2)}, u32[]{:S(2)}) collective-permute-start(f32[2,512]{1,0:T(2,128)S(1)} %multiply_add_fusion.19), channel_id=1, source_target_pairs={{0,8},{8,16},{16,24},{24,32},{32,40},{40,48},{48,56},{56,64},{64,7... | collective-permute-start | bytes 12296 | tf_op jit(solution)/shard_map/while/body/eval_jaxpr/ppermute | solution.py:10
  263.3 7.9 %collective-permute-start = (f32[2,512]{1,0:T(2,128)S(1)}, f32[2,512]{1,0:T(2,128)S(1)}, u32[]{:S(2)}, u32[]{:S(2)}) collective-permute-start(f32[2,512]{1,0:T(2,128)S(1)} %multiply_add_fusion.18), channel_id=1, source_target_pairs={{8,0},{16,8},{24,16},{32,24},{40,32},{48,40},{56,48},{64,56},{72,6... | collective-permute-start | bytes 12296 | tf_op jit(solution)/shard_map/while/body/eval_jaxpr/ppermute | solution.py:10
  278.3 7.9 %collective-permute-start = (f32[2,512]{1,0:T(2,128)S(1)}, f32[2,512]{1,0:T(2,128)S(1)}, u32[]{:S(2)}, u32[]{:S(2)}) collective-permute-start(f32[2,512]{1,0:T(2,128)S(1)} %multiply_add_fusion.18), channel_id=1, source_target_pairs={{8,0},{16,8},{24,16},{32,24},{40,32},{48,40},{56,48},{64,56},{72,6... | collective-permute-start | bytes 12296 | tf_op jit(solution)/shard_map/while/body/eval_jaxpr/ppermute | solution.py:10
  286.2 7.3 %collective-permute-start = (f32[2,512]{1,0:T(2,128)S(1)}, f32[2,512]{1,0:T(2,128)S(1)}, u32[]{:S(2)}, u32[]{:S(2)}) collective-permute-start(f32[2,512]{1,0:T(2,128)S(1)} %multiply_add_fusion.18), channel_id=1, source_target_pairs={{8,0},{16,8},{24,16},{32,24},{40,32},{48,40},{56,48},{64,56},{72,6... | collective-permute-start | bytes 12296 | tf_op jit(solution)/shard_map/while/body/eval_jaxpr/ppermute | solution.py:10
  293.5 7.3 %collective-permute-start = (f32[2,512]{1,0:T(2,128)S(1)}, f32[2,512]{1,0:T(2,128)S(1)}, u32[]{:S(2)}, u32[]{:S(2)}) collective-permute-start(f32[2,512]{1,0:T(2,128)S(1)} %multiply_add_fusion.18), channel_id=1, source_target_pairs={{8,0},{16,8},{24,16},{32,24},{40,32},{48,40},{56,48},{64,56},{72,6... | collective-permute-start | bytes 12296 | tf_op jit(solution)/shard_map/while/body/eval_jaxpr/ppermute | solution.py:10
  300.9 7.3 %collective-permute-start = (f32[2,512]{1,0:T(2,128)S(1)}, f32[2,512]{1,0:T(2,128)S(1)}, u32[]{:S(2)}, u32[]{:S(2)}) collective-permute-start(f32[2,512]{1,0:T(2,128)S(1)} %multiply_add_fusion.18), channel_id=1, source_target_pairs={{8,0},{16,8},{24,16},{32,24},{40,32},{48,40},{56,48},{64,56},{72,6... | collective-permute-start | bytes 12296 | tf_op jit(solution)/shard_map/while/body/eval_jaxpr/ppermute | solution.py:10
  308.2 7.3 %collective-permute-start = (f32[2,512]{1,0:T(2,128)S(1)}, f32[2,512]{1,0:T(2,128)S(1)}, u32[]{:S(2)}, u32[]{:S(2)}) collective-permute-start(f32[2,512]{1,0:T(2,128)S(1)} %multiply_add_fusion.18), channel_id=1, source_target_pairs={{8,0},{16,8},{24,16},{32,24},{40,32},{48,40},{56,48},{64,56},{72,6... | collective-permute-start | bytes 12296 | tf_op jit(solution)/shard_map/while/body/eval_jaxpr/ppermute | solution.py:10
  315.5 7.3 %collective-permute-start = (f32[2,512]{1,0:T(2,128)S(1)}, f32[2,512]{1,0:T(2,128)S(1)}, u32[]{:S(2)}, u32[]{:S(2)}) collective-permute-start(f32[2,512]{1,0:T(2,128)S(1)} %multiply_add_fusion.18), channel_id=1, source_target_pairs={{8,0},{16,8},{24,16},{32,24},{40,32},{48,40},{56,48},{64,56},{72,6... | collective-permute-start | bytes 12296 | tf_op jit(solution)/shard_map/while/body/eval_jaxpr/ppermute | solution.py:10
  322.8 7.3 %collective-permute-start = (f32[2,512]{1,0:T(2,128)S(1)}, f32[2,512]{1,0:T(2,128)S(1)}, u32[]{:S(2)}, u32[]{:S(2)}) collective-permute-start(f32[2,512]{1,0:T(2,128)S(1)} %multiply_add_fusion.18), channel_id=1, source_target_pairs={{8,0},{16,8},{24,16},{32,24},{40,32},{48,40},{56,48},{64,56},{72,6... | collective-permute-start | bytes 12296 | tf_op jit(solution)/shard_map/while/body/eval_jaxpr/ppermute | solution.py:10
  330.2 7.3 %collective-permute-start = (f32[2,512]{1,0:T(2,128)S(1)}, f32[2,512]{1,0:T(2,128)S(1)}, u32[]{:S(2)}, u32[]{:S(2)}) collective-permute-start(f32[2,512]{1,0:T(2,128)S(1)} %multiply_add_fusion.18), channel_id=1, source_target_pairs={{8,0},{16,8},{24,16},{32,24},{40,32},{48,40},{56,48},{64,56},{72,6... | collective-permute-start | bytes 12296 | tf_op jit(solution)/shard_map/while/body/eval_jaxpr/ppermute | solution.py:10
  337.5 7.3 %collective-permute-start = (f32[2,512]{1,0:T(2,128)S(1)}, f32[2,512]{1,0:T(2,128)S(1)}, u32[]{:S(2)}, u32[]{:S(2)}) collective-permute-start(f32[2,512]{1,0:T(2,128)S(1)} %multiply_add_fusion.18), channel_id=1, source_target_pairs={{8,0},{16,8},{24,16},{32,24},{40,32},{48,40},{56,48},{64,56},{72,6... | collective-permute-start | bytes 12296 | tf_op jit(solution)/shard_map/while/body/eval_jaxpr/ppermute | solution.py:10
  344.8 7.3 %collective-permute-start = (f32[2,512]{1,0:T(2,128)S(1)}, f32[2,512]{1,0:T(2,128)S(1)}, u32[]{:S(2)}, u32[]{:S(2)}) collective-permute-start(f32[2,512]{1,0:T(2,128)S(1)} %multiply_add_fusion.18), channel_id=1, source_target_pairs={{8,0},{16,8},{24,16},{32,24},{40,32},{48,40},{56,48},{64,56},{72,6... | collective-permute-start | bytes 12296 | tf_op jit(solution)/shard_map/while/body/eval_jaxpr/ppermute | solution.py:10
  352.1 7.3 %collective-permute-start = (f32[2,512]{1,0:T(2,128)S(1)}, f32[2,512]{1,0:T(2,128)S(1)}, u32[]{:S(2)}, u32[]{:S(2)}) collective-permute-start(f32[2,512]{1,0:T(2,128)S(1)} %multiply_add_fusion.18), channel_id=1, source_target_pairs={{8,0},{16,8},{24,16},{32,24},{40,32},{48,40},{56,48},{64,56},{72,6... | collective-permute-start | bytes 12296 | tf_op jit(solution)/shard_map/while/body/eval_jaxpr/ppermute | solution.py:10
  359.5 7.3 %collective-permute-start = (f32[2,512]{1,0:T(2,128)S(1)}, f32[2,512]{1,0:T(2,128)S(1)}, u32[]{:S(2)}, u32[]{:S(2)}) collective-permute-start(f32[2,512]{1,0:T(2,128)S(1)} %multiply_add_fusion.18), channel_id=1, source_target_pairs={{8,0},{16,8},{24,16},{32,24},{40,32},{48,40},{56,48},{64,56},{72,6... | collective-permute-start | bytes 12296 | tf_op jit(solution)/shard_map/while/body/eval_jaxpr/ppermute | solution.py:10
  366.8 7.3 %collective-permute-start = (f32[2,512]{1,0:T(2,128)S(1)}, f32[2,512]{1,0:T(2,128)S(1)}, u32[]{:S(2)}, u32[]{:S(2)}) collective-permute-start(f32[2,512]{1,0:T(2,128)S(1)} %multiply_add_fusion.18), channel_id=1, source_target_pairs={{8,0},{16,8},{24,16},{32,24},{40,32},{48,40},{56,48},{64,56},{72,6... | collective-permute-start | bytes 12296 | tf_op jit(solution)/shard_map/while/body/eval_jaxpr/ppermute | solution.py:10
  383.6 181.8 %reduce-scatter.5.cloned.1.call-start = ((), (), s32[]{:S(2)}) async-start(), calls=%async_computation.4 | async-start | bytes 7077888 | tf_op jit(solution)/shard_map/reduce_scatter | solution.py:64
  (28 other events, 263.7 us)
Sparse Core Ops, SparseCore 0:
  9.6 44.7 all-gather.1
  383.7 106.2 reduce-scatter.2
  492.4 72.9 reduce-scatter.4
where the time goes:
time: 577 us; the launch traced here: 574 us
  waiting for transfers between devices  307 us (53%)
  starting transfers between devices  121 us (21%)
  local copies, waits for them, and re-layouts  67.6 us (12%)
  other arithmetic  38.2 us (7%)
  matrix products  25.4 us (4%)
  between operations  15 us (3%)
    ppermute x30, starting transfers between devices, from_behind(): return lax.ppermute(block, axis, route)  121 us
    reduce_scatter x1, waiting for transfers between devices, shards(): lax.psum_scatter(lax.dot_general(flat, deltas, (((0,), (0,)), ((), ())),...  97.4 us
    ppermute x30, waiting for transfers between devices, from_behind(): return lax.ppermute(block, axis, route)  92.8 us
    reduce_scatter x1, waiting for transfers between devices, shards(): lax.psum_scatter(term, 'tp', scatter_dimension=2, tiled=True)  72.3 us
    all_gather x1, waiting for transfers between devices, shards(): whole = lax.all_gather(tokens, 'tp', axis=2, tiled=True)  43.2 us
    slice x47, local copies, waits for them, and re-layouts, shards(): lax.associative_scan(compose, (keep, (1.0 - keep) * cand), axis=1)  20.1 us
    slice x53, local copies, waits for them, and re-layouts, shards(): lax.associative_scan(compose, (coef, score), reverse=True, axis=1)  16.9 us
  transfers between devices with their start and end apart: 33, of which 33 were waited for; matrix products, arithmetic and copies ran while one was open for 3% of the time, Pallas kernels for 0%

commit v1 on v0

v1 whole, which is shorter than its diff:
```python
import functools

import jax
import jax.numpy as jnp
from jax import lax
from jax.experimental import pallas as pl
from jax.experimental.pallas import tpu as pltpu
from jax.sharding import PartitionSpec as P


BF16 = jnp.bfloat16
F32 = jnp.float32
AXES = ("seq", "tp")
ZS, HS, CS, LS, YS = 4, 2, 2, 2, 4
TPS = LS * YS
CHUNKS = 8
LANES = 128
EARLY = 5
SPLIT = 640
BLOCKS = ((0, 0), (0, 3), (0, 1), (1, 0), (0, 2), (1, 3), (1, 1), (1, 2))
LIMIT = 8 << 20


def move(block, dz=0, dh=0, dc=0, dl=0, dy=0):
    route = []
    for z in range(ZS):
        for h in range(HS):
            for c in range(CS):
                for l in range(LS):
                    for y in range(YS):
                        source = (((z * HS + h) * CS + c) * LS + l) * YS + y
                        target = ((((z + dz) % ZS * HS + (h + dh) % HS) * CS + (c + dc) % CS) * LS + (l + dl) % LS) * YS + (y + dy) % YS
                        route.append((source, target))
    return lax.ppermute(block, AXES, route)


def take(ref, rows):
    return jnp.concatenate([ref[q, rows, :] for q in range(ref.shape[0])], axis=1)


def put(ref, rows, value):
    for q in range(ref.shape[0]):
        ref[q, rows, :] = value[:, q * LANES : (q + 1) * LANES]


def feature(coords, dl, dy):
    return lax.rem(coords[3] + dl, LS) * YS + lax.rem(coords[4] + dy, YS)


def slot(coords, dz, dh):
    want = lax.rem(coords[0] + dz, ZS) * HS + lax.rem(coords[1] + dh, HS)
    dl = lax.rem(lax.div(want, YS) + LS - coords[3], LS)
    return dl * YS + lax.rem(lax.rem(want, YS) + YS - coords[4], YS)


def joined(blocks):
    return jnp.concatenate([ref[...] for ref in blocks], axis=1)


def fetch(weights, block, rows, slot, sems):
    size, wide = rows.shape[1:]
    copies = []
    for side, w in enumerate(weights):
        source = w.at[pl.ds(pl.multiple_of(block * size, size), size), :]
        target = rows.at[slot, :, pl.ds(side * (wide // 2), wide // 2)]
        copies.append(pltpu.make_async_copy(source, target, sems.at[slot, side]))
    for copy in copies:
        copy.start()
    return copies


def early_kernel(coords, *refs):
    blocks = refs[:EARLY]
    wg, wc, acc, rest, rows, sems, rest_sems = refs[EARLY:]
    size, wide = rows.shape[1:]
    copies = [fetch((wg, wc), feature(coords, *BLOCKS[i]), rows, i, sems) for i in range(EARLY)]
    rest_copies = [fetch((wg, wc), feature(coords, *BLOCKS[EARLY + i]), rest, i, rest_sems) for i in range(TPS - EARLY)]
    for pair in copies:
        for copy in pair:
            copy.wait()
    acc[...] = jnp.dot(joined(blocks), rows[...].reshape(EARLY * size, wide), preferred_element_type=F32)
    for pair in rest_copies:
        for copy in pair:
            copy.wait()


def late_kernel(*refs):
    count = TPS - EARLY
    rows, bias, score, start = refs[count : count + 4]
    keep_out, cand_out, score_out, sums_out, span_out = refs[count + 4 : count + 9]
    acc_g, acc_c, scores = refs[count + 9 :]
    size, wide = rows.shape[1:]
    spread = rows[...].reshape(count * size, wide)
    both = start[...] + jnp.dot(joined(refs[:count]), spread, preferred_element_type=F32)
    g, c = both[:, : wide // 2], both[:, wide // 2 :]
    for q in range(scores.shape[0]):
        lanes = slice(q * LANES, (q + 1) * LANES)
        acc_g[q] = g[:, lanes]
        acc_c[q] = c[:, lanes]
        scores[q] = score[:, lanes]
    batch, steps, _, width = keep_out.shape
    length = steps * CHUNKS
    shift = bias[...]
    for b in range(batch):
        prod = jnp.ones((CHUNKS, width), F32)
        state = jnp.zeros((CHUNKS, width), F32)
        for j in range(steps):
            rows = pl.ds(b * length + j, CHUNKS, stride=steps)
            keep = jax.nn.sigmoid(take(acc_g, rows) + shift)
            cand = take(acc_c, rows)
            keep_out[b, j] = keep
            cand_out[b, j] = cand
            prod = prod * keep
            state = keep * state + (1.0 - keep) * cand
        back = jnp.zeros((CHUNKS, width), F32)
        for j in reversed(range(steps)):
            rows = pl.ds(b * length + j, CHUNKS, stride=steps)
            pull = take(scores, rows)
            score_out[b, j] = pull
            back = keep_out[b, j] * (pull + back)
        sums_out[b, 0] = prod
        sums_out[b, 1] = state
        sums_out[b, 2] = back
        whole = prod[0:1]
        ahead = state[0:1]
        for c in range(1, CHUNKS):
            whole = whole * prod[c : c + 1]
            ahead = prod[c : c + 1] * ahead + state[c : c + 1]
        behind = back[CHUNKS - 1 : CHUNKS]
        for c in reversed(range(CHUNKS - 1)):
            behind = back[c : c + 1] + prod[c : c + 1] * behind
        span_out[4 * b : 4 * b + 1] = whole
        span_out[4 * b + 1 : 4 * b + 2] = ahead
        span_out[4 * b + 2 : 4 * b + 3] = behind
        span_out[4 * b + 3 : 4 * b + 4] = jnp.zeros_like(whole)


def cost(flops):
    return pl.CostEstimate(flops=3 * flops, transcendentals=0, bytes_accessed=0)


def local(kernel, inputs, out_shape, scratch=(), flops=0, scalars=1, remote=0):
    vmem = pl.BlockSpec(memory_space=pltpu.VMEM)
    return pl.pallas_call(
        kernel,
        in_specs=[pl.BlockSpec(memory_space=pltpu.SMEM)] * scalars + [vmem] * (len(inputs) - scalars - remote) + [pl.BlockSpec(memory_space=pltpu.HBM)] * remote,
        out_specs=jax.tree.map(lambda _: vmem, out_shape),
        out_shape=out_shape,
        scratch_shapes=list(scratch),
        compiler_params=pltpu.CompilerParams(vmem_limit_bytes=LIMIT),
        cost_estimate=cost(flops),
    )(*inputs)


def early(coords, blocks, wg, wc):
    count, (rows, block) = len(blocks), blocks[0].shape
    wide = 2 * wg.shape[1]
    return local(
        early_kernel,
        (coords, *blocks, wg, wc),
        [jax.ShapeDtypeStruct((rows, wide), F32), jax.ShapeDtypeStruct((TPS - count, block, wide), BF16)],
        [pltpu.VMEM((count, block, wide), BF16), pltpu.SemaphoreType.DMA((count, 2)), pltpu.SemaphoreType.DMA((TPS - count, 2))],
        flops=2 * rows * block * wide * count,
        remote=2,
    )


def late(blocks, spread, bias, score, start, batch):
    rows, block = blocks[0].shape
    width = bias.shape[1]
    tall = jax.ShapeDtypeStruct((batch, rows // batch // CHUNKS, CHUNKS, width), F32)
    sums = jax.ShapeDtypeStruct((batch, 3, CHUNKS, width), F32)
    span = jax.ShapeDtypeStruct((4 * batch, width), F32)
    return local(
        late_kernel,
        (*blocks, spread, bias, score, start),
        [tall, tall, tall, sums, span],
        [pltpu.VMEM((width // LANES, rows, LANES), F32)] * 3,
        flops=4 * rows * block * width * len(blocks),
        scalars=0,
    )


def arrange_kernel(coords, *refs):
    mine, theirs = refs[TPS:]
    half = mine.shape[2]
    for i in range(TPS):
        low, high = refs[i][:, :half], refs[i][:, half:]
        mine[i] = jnp.where(coords[2] == 0, low, high)
        theirs[i] = jnp.where(coords[2] == 0, high, low)


def arrange(coords, blocks):
    rows, block = blocks[0].shape
    half = jax.ShapeDtypeStruct((TPS, rows, block // CS), BF16)
    return local(arrange_kernel, (coords, *blocks), [half, half], flops=1 << 27)


def backward_kernel(place, keep_in, cand_in, sums, score, spans, deltas, before, tail, head, pres, cands):
    batch, steps, _, width = keep_in.shape
    length = steps * CHUNKS
    z, h, c = place[0], place[1], place[2]
    mine = (z * HS + h) * CS + c
    order = [(i // (HS * CS), i // CS % HS, i % CS) for i in range(ZS * HS * CS)]

    def span(i):
        oz, oh, oc = order[i]
        slot = (lax.rem(oz - z + ZS, ZS) * HS + lax.rem(oh + h, HS)) * CS + lax.rem(oc + c, CS)
        return spans[slot]

    for b in range(batch):
        into = jnp.zeros((1, width), F32)
        for i in range(len(order) - 1):
            s = span(i)
            into = jnp.where(i < mine, s[4 * b : 4 * b + 1] * into + s[4 * b + 1 : 4 * b + 2], into)
        back = jnp.zeros((1, width), F32)
        for i in reversed(range(1, len(order))):
            s = span(i)
            back = jnp.where(i > mine, s[4 * b : 4 * b + 1] * back + s[4 * b + 2 : 4 * b + 3], back)
        for k in range(CHUNKS):
            head[k : k + 1] = into
            into = sums[b, 0, k : k + 1] * into + sums[b, 1, k : k + 1]
        for k in reversed(range(CHUNKS)):
            tail[k : k + 1] = back
            back = sums[b, 0, k : k + 1] * back + sums[b, 2, k : k + 1]
        state = head[...]
        for j in range(steps):
            before[j] = state
            keep = keep_in[b, j]
            state = keep * state + (1.0 - keep) * cand_in[b, j]
        carry = tail[...]
        for j in reversed(range(steps)):
            rows = pl.ds(b * length + j, CHUNKS, stride=steps)
            keep = keep_in[b, j]
            adjoint = score[b, j] + carry
            fresh = adjoint * (1.0 - keep)
            put(pres, rows, fresh * keep * (before[j] - cand_in[b, j]))
            put(cands, rows, fresh)
            carry = keep * adjoint
    for q in range(width // LANES):
        deltas[:, q * LANES : (q + 1) * LANES] = pres[q].astype(BF16)
        deltas[:, width + q * LANES : width + (q + 1) * LANES] = cands[q].astype(BF16)


def backward(place, keep, cand, sums, score, spans):
    batch, steps, _, width = keep.shape
    rows = batch * steps * CHUNKS
    return local(
        backward_kernel,
        (place, keep, cand, sums, score, spans),
        jax.ShapeDtypeStruct((rows, 2 * width), BF16),
        [pltpu.VMEM((steps, CHUNKS, width), F32)]
        + [pltpu.VMEM((CHUNKS, width), F32)] * 2
        + [pltpu.VMEM((width // LANES, rows, LANES), F32)] * 2,
        flops=1 << 28,
    )


def weights_kernel(coords, own, other, d_own, d_other, *outs, spots, low, high):
    half = own.shape[2]
    slots = [slot(coords, *spot) for spot in spots]
    lhs = jnp.concatenate([jnp.concatenate([own[i], other[i]], axis=0) for i in slots], axis=1)
    rhs = jnp.concatenate([d_own[:, low:high], d_other[:, low:high]], axis=0)
    total = lax.dot_general(lhs, rhs, (((0,), (0,)), ((), ())), preferred_element_type=F32)
    for i, out in enumerate(outs):
        out[...] = total[i * half : (i + 1) * half].astype(BF16)


def weights(coords, spots, own, other, d_own, d_other, low, high):
    count = len(spots)
    rows, half = own.shape[1:]
    return local(
        functools.partial(weights_kernel, spots=spots, low=low, high=high),
        (coords, own, other, d_own, d_other),
        [jax.ShapeDtypeStruct((half, high - low), BF16)] * count,
        flops=4 * rows * half * count * (high - low),
    )


def rows_kernel(coords, wg, wc, rows, sems):
    copies = [fetch((wg, wc), feature(coords, *BLOCKS[i]), rows, i, sems) for i in range(TPS)]
    for pair in copies:
        for copy in pair:
            copy.wait()


def weight_rows(coords, wg, wc, block):
    return local(
        rows_kernel,
        (coords, wg, wc),
        jax.ShapeDtypeStruct((TPS, block, 2 * wg.shape[1]), BF16),
        [pltpu.SemaphoreType.DMA((TPS, 2))],
        flops=1 << 27,
        remote=2,
    )


def inputs_kernel(deltas, rows, *outs, spots):
    for spot, out in zip(spots, outs, strict=True):
        weight = rows[BLOCKS.index(spot)]
        total = lax.dot_general(deltas[...], weight, (((1,), (1,)), ((), ())), preferred_element_type=F32)
        out[...] = total.astype(BF16)


def inputs(spots, deltas, rows):
    count, wide = deltas.shape
    block = rows.shape[1]
    return local(
        functools.partial(inputs_kernel, spots=spots),
        (deltas, rows),
        [jax.ShapeDtypeStruct((count, block), BF16)] * len(spots),
        flops=2 * count * wide * block * len(spots),
        scalars=0,
    )


def plus(*parts):
    total = parts[0].astype(F32)
    for part in parts[1:]:
        total = total + part.astype(F32)
    return total


def layer(tokens, gate_weight, cand_weight, forget_bias, readout, advantage):
    batch, count, block = tokens.shape
    width = gate_weight.shape[1]
    rows = batch * count
    seq = lax.axis_index("seq")
    tp = lax.axis_index("tp")
    places = [lax.div(seq, HS * CS), lax.rem(lax.div(seq, CS), HS), lax.rem(seq, CS), lax.div(tp, YS), lax.rem(tp, YS)]
    coords = jnp.stack(places).astype(jnp.int32)
    gate_weight = pltpu.with_memory_space_constraint(gate_weight, pltpu.HBM)
    cand_weight = pltpu.with_memory_space_constraint(cand_weight, pltpu.HBM)

    own = tokens.reshape(rows, block)
    part = rows // 2
    lower = move(own, dy=1)
    upper = move(own, dy=-1)
    across = move(own, dl=1)
    far = jnp.concatenate([move(lower[:part], dy=1), move(upper[part:], dy=-1)], axis=0)
    across_lower = move(across, dy=1)
    across_upper = move(across, dy=-1)
    across_far = move(far, dl=1)
    blocks = [own, lower, upper, across, far, across_lower, across_upper, across_far]
    score = ((advantage.astype(F32) * 0.25)[:, :, None] * readout.astype(F32)).reshape(rows, width)
    start, spread = early(coords, blocks[:EARLY], gate_weight, cand_weight)
    keep, cand, pull, sums, span = late(blocks[EARLY:], spread, forget_bias.reshape(1, width), score, start, batch)

    spans = jnp.stack([span, move(span, dc=1)])
    ordered = [own, upper, far, lower, across, across_upper, across_far, across_lower]
    mine, theirs = arrange(coords, ordered)
    weight_block = weight_rows(coords, gate_weight, cand_weight, block)
    others = move(theirs, dc=1)
    spans = jnp.concatenate([spans, move(spans, dh=1)])
    spans = jnp.concatenate([spans, move(spans, dz=-1), move(spans, dz=2), move(spans, dz=1)])
    deltas = backward(coords, keep, cand, sums, pull, spans)

    their_deltas = move(deltas, dc=1)
    t_grads = lambda *spots: inputs(spots, deltas, weight_block)
    t_far = t_grads((0, 2), (1, 2))
    t_lower = move(t_far[0], dy=1)
    t_upper = move(t_far[1], dy=-1)

    grads = lambda spots, low, high: weights(coords, spots, mine, others, deltas, their_deltas, low, high)
    wide = 2 * width
    opposite = grads([(2, 0), (2, 1)], 0, SPLIT)
    met_lower = move(opposite[0], dz=1)
    met_upper = move(opposite[1], dz=-1)
    pair_out = move(jnp.stack(grads([(0, 1), (1, 1), (2, 1), (3, 1)], SPLIT, wide)), dh=1)
    t_near = t_grads((0, 1), (1, 1), (0, 3), (1, 3))
    nearby = grads([(1, 0), (1, 1), (3, 0), (3, 1)], 0, SPLIT)
    t_near += t_grads((1, 0), (0, 0))
    nearby += grads([(0, 1), (0, 0)], 0, SPLIT)
    pair_own = grads([(0, 0), (1, 0), (2, 0), (3, 0)], SPLIT, wide)

    u_lower = move(jnp.stack([plus(t_near[0], t_lower).astype(BF16), t_near[1]]), dy=1)
    u_upper = move(jnp.stack([t_near[2], plus(t_near[3], t_upper).astype(BF16)]), dy=-1)
    from_lower = move(jnp.stack([plus(nearby[0], met_lower).astype(BF16), nearby[1]]), dz=1)
    from_upper = move(jnp.stack([nearby[2], plus(nearby[3], met_upper).astype(BF16)]), dz=-1)
    t_pair = move(plus(t_near[4], u_lower[1], u_upper[1]).astype(BF16), dl=1)
    from_pair = move(plus(nearby[4], from_lower[1], from_upper[1]).astype(BF16), dh=1)
    pair = [plus(pair_own[i], pair_out[i]) for i in range(ZS)]
    pair_in = [move(pair[i].astype(BF16), dz=i) for i in range(1, ZS)]
    left = plus(nearby[5], from_lower[0], from_upper[0], from_pair)
    right = plus(pair[0], *pair_in)
    grad_gate = left[:, :width]
    grad_cand = jnp.concatenate([left[:, width:], right], axis=1)
    grad_tokens = plus(t_near[5], u_lower[0], u_upper[0], t_pair).astype(BF16).reshape(batch, count, block)
    return (grad_gate, grad_cand, grad_tokens)


def solution(mesh):
    in_specs = (
        P(None, "seq", "tp"),
        P(None, "tp"),
        P(None, "tp"),
        P("tp"),
        P(None, "seq", "tp"),
        P(None, "seq"),
    )
    out_specs = (P("seq", "tp"), P("seq", "tp"), P(None, "seq", "tp"))
    return jax.shard_map(layer, mesh=mesh, in_specs=in_specs, out_specs=out_specs, check_vma=False)
```

time: 577 us -> 118 us (0.20)
  the two profiles are of different devices: /device:TPU:1 before, /device:TPU:4 now
where the time goes in v1:
time: 118 us
  waiting for transfers between devices  46 us (39%)
  starting transfers between devices  38.1 us (32%)
  Pallas kernels  26.3 us (22%)
  other arithmetic  5.1 us (4%)
    ppermute x29, waiting for transfers between devices, move(): return lax.ppermute(block, AXES, route)  46 us
    ppermute x29, starting transfers between devices, move(): return lax.ppermute(block, AXES, route)  38.1 us
    pallas_call x13, Pallas kernels, local(): pl.pallas_call(kernel, in_specs=[pl.BlockSpec(memory_space=pltpu.SMEM)] *...  26.3 us
  transfers between devices with their start and end apart: 29, of which 13 were waited for; matrix products, arithmetic and copies ran while one was open for 4% of the time, Pallas kernels for 21%

profile of v1, /device:TPU:4, one launch (start us, length us, event | category | flops | bytes accessed | tf_op | source)
XLA Modules:
  0.0 117.5 jit_solution(8111755616703297137)
XLA Ops:
  2.3 1.7 %collective-permute-start = (bf16[384,512]{1,0:T(8,128)(2,1)}, bf16[384,512]{1,0:T(8,128)(2,1)S(1)}, u32[]{:S(2)}, u32[]{:S(2)}) collective-permute-start(bf16[384,512]{1,0:T(8,128)(2,1)} %bitcast.93), channel_id=1, source_target_pairs={{0,3},{1,0},{2,1},{3,2},{4,7},{5,4},{6,5},{7,6},{8,11},{9,8},{10,9... | collective-permute-start | bytes 1179656 | tf_op jit(solution)/shard_map/ppermute | solution.py:34
  5.8 7.2 %collective-permute-done.1.refs_3_.refs_1_ = bf16[384,512]{1,0:T(8,128)(2,1)S(1)} collective-permute-done((bf16[384,512]{1,0:T(8,128)(2,1)}, bf16[384,512]{1,0:T(8,128)(2,1)S(1)}, u32[]{:S(2)}, u32[]{:S(2)}) %collective-permute-start.1) | collective-permute-done | bytes 393248 | tf_op jit(solution)/shard_map/ppermute | solution.py:34
  13.4 3.0 %collective-permute-start.3 = (bf16[192,512]{1,0:T(8,128)(2,1)S(1)}, bf16[192,512]{1,0:T(8,128)(2,1)S(1)}, u32[]{:S(2)}, u32[]{:S(2)}) collective-permute-start(bf16[192,512]{1,0:T(8,128)(2,1)S(1)} %slice.65), channel_id=1, source_target_pairs={{0,3},{1,0},{2,1},{3,2},{4,7},{5,4},{6,5},{7,6},{8,11},{9,8},{10,9... | collective-permute-start | bytes 589832 | tf_op jit(solution)/shard_map/ppermute | solution.py:34
  17.7 4.1 %shard_map.94.rows = bf16[8,512,1024]{2,1,0:T(8,128)(2,1)S(1)} custom-call(s32[5]{0:T(128)S(1)} %stack.83.coords.place, bf16[4096,512]{1,0:T(8,128)(2,1)} %wg.1, bf16[4096,512]{1,0:T(8,128)(2,1)} %wc.1), custom_call_target="tpu_custom_call" | custom-call | flops 402653184 | tf_op jit(solution)/shard_map/pallas_call | solution.py:144
  21.8 3.2 %collective-permute-start.5 = (bf16[384,512]{1,0:T(8,128)(2,1)S(1)}, bf16[384,512]{1,0:T(8,128)(2,1)S(1)}, u32[]{:S(2)}, u32[]{:S(2)}) collective-permute-start(bf16[384,512]{1,0:T(8,128)(2,1)S(1)} %collective-permute-done.4.refs_4_.refs_3_), channel_id=1, source_target_pairs={{0,3},{1,0},{2,1},{3,2},{4,7},{5,4},{6,5},{7,6},{8,11},{9,8},{10,9... | collective-permute-start | bytes 1179656 | tf_op jit(solution)/shard_map/ppermute | solution.py:34
  26.4 6.1 %shard_map.86 = (f32[384,1024]{1,0:T(8,128)S(1)}, bf16[3,512,1024]{2,1,0:T(8,128)(2,1)S(1)}) custom-call(s32[5]{0:T(128)S(1)} %stack.83.coords.place, bf16[384,512]{1,0:T(8,128)(2,1)S(1)} %bitcast.95, bf16[384,512]{1,0:T(8,128)(2,1)S(1)} %collective-permute-done.1.refs_3_.refs_1_, bf16[384,512]{1,0:T(8,128)(2,1)S(1)} %collective-permute-done.refs_1_.refs_2_, ...), custom_call_target="tpu_custom_call" | custom-call | flops 6039797760 | tf_op jit(solution)/shard_map/pallas_call | solution.py:144
  34.2 2.0 %shard_map.87 = (f32[2,24,8,512]{3,2,1,0:T(8,128)S(1)}, f32[2,24,8,512]{3,2,1,0:T(8,128)S(1)}, f32[2,24,8,512]{3,2,1,0:T(8,128)S(1)}, f32[2,3,8,512]{3,2,1,0:T(8,128)S(1)}, f32[8,512]{1,0:T(8,128)S(1)}) custom-call(bf16[384,512]{1,0:T(8,128)(2,1)S(1)} %collective-permute-done.7.refs_7_.refs_0_, bf16[384,512]{1,0:T(8,128)(2,1)S(1)} %collective-permute-done.5.refs_5_.refs_1_, ...), custom_call_target="tpu_custom_call" | custom-call | flops 3623878656 | tf_op jit(solution)/shard_map/pallas_call | solution.py:144
  38.3 4.8 %collective-permute-done.10 = f32[2,8,512]{2,1,0:T(8,128)S(1)} collective-permute-done((f32[2,8,512]{2,1,0:T(8,128)S(1)}, f32[2,8,512]{2,1,0:T(8,128)S(1)}, u32[]{:S(2)}, u32[]{:S(2)}) %collective-permute-start.10) | collective-permute-done | bytes 32800 | tf_op jit(solution)/shard_map/ppermute | solution.py:34
  43.1 1.9 %collective-permute-start.13 = (f32[4,8,512]{2,1,0:T(8,128)S(1)}, f32[4,8,512]{2,1,0:T(8,128)S(1)}, u32[]{:S(2)}, u32[]{:S(2)}) collective-permute-start(f32[4,8,512]{2,1,0:T(8,128)S(1)} %pad_maximum_fusion.6), channel_id=1, source_target_pairs={{0,32},{1,33},{2,34},{3,35},{4,36},{5,37},{6,38},{7,39},{8,40},{9,... | collective-permute-start | bytes 196616 | tf_op jit(solution)/shard_map/ppermute | solution.py:34
  45.0 3.6 %collective-permute-start.12 = (f32[4,8,512]{2,1,0:T(8,128)S(1)}, f32[4,8,512]{2,1,0:T(8,128)S(1)}, u32[]{:S(2)}, u32[]{:S(2)}) collective-permute-start(f32[4,8,512]{2,1,0:T(8,128)S(1)} %pad_maximum_fusion.6), channel_id=1, source_target_pairs={{0,64},{1,65},{2,66},{3,67},{4,68},{5,69},{6,70},{7,71},{8,72},{9,... | collective-permute-start | bytes 196616 | tf_op jit(solution)/shard_map/ppermute | solution.py:34
  49.6 3.2 %collective-permute-done.11 = f32[4,8,512]{2,1,0:T(8,128)S(1)} collective-permute-done((f32[4,8,512]{2,1,0:T(8,128)S(1)}, f32[4,8,512]{2,1,0:T(8,128)S(1)}, u32[]{:S(2)}, u32[]{:S(2)}) %collective-permute-start.11) | collective-permute-done | bytes 65568 | tf_op jit(solution)/shard_map/ppermute | solution.py:34
  56.9 1.9 %shard_map.96 = (bf16[384,512]{1,0:T(8,128)(2,1)S(1)}, bf16[384,512]{1,0:T(8,128)(2,1)S(1)}, bf16[384,512]{1,0:T(8,128)(2,1)S(1)}, bf16[384,512]{1,0:T(8,128)(2,1)S(1)}) custom-call(bf16[384,1024]{1,0:T(8,128)(2,1)S(1)} %shard_map.88.d_own.deltas, bf16[8,512,1024]{2,1,0:T(8,128)(2,1)S(1)} %shard_map.94.rows), custom_call_target="tpu_custom_call" | custom-call | flops 4831838208 | tf_op jit(solution)/shard_map/pallas_call | solution.py:144
  60.8 6.3 %collective-permute-done.26 = bf16[384,512]{1,0:T(8,128)(2,1)S(1)} collective-permute-done((bf16[384,512]{1,0:T(8,128)(2,1)S(1)}, bf16[384,512]{1,0:T(8,128)(2,1)S(1)}, u32[]{:S(2)}, u32[]{:S(2)}) %collective-permute-start.26) | collective-permute-done | bytes 393248 | tf_op jit(solution)/shard_map/ppermute | solution.py:34
  67.3 2.6 %collective-permute-start.27 = (bf16[2,384,512]{2,1,0:T(8,128)(2,1)S(1)}, bf16[2,384,512]{2,1,0:T(8,128)(2,1)S(1)}, u32[]{:S(2)}, u32[]{:S(2)}) collective-permute-start(bf16[2,384,512]{2,1,0:T(8,128)(2,1)S(1)} %pad_maximum_fusion.2), channel_id=1, source_target_pairs={{0,3},{1,0},{2,1},{3,2},{4,7},{5,4},{6,5},{7,6},{8,11},{9,8},{10,9... | collective-permute-start | bytes 2359304 | tf_op jit(solution)/shard_map/ppermute | solution.py:34
  73.4 3.1 %collective-permute-start.17 = (bf16[256,640]{1,0:T(8,128)(2,1)S(1)}, bf16[256,640]{1,0:T(8,128)(2,1)S(1)}, u32[]{:S(2)}, u32[]{:S(2)}) collective-permute-start(bf16[256,640]{1,0:T(8,128)(2,1)S(1)} %get-tuple-element.51), channel_id=1, source_target_pairs={{0,96},{1,97},{2,98},{3,99},{4,100},{5,101},{6,102},{7,103},{8,104... | collective-permute-start | bytes 983048 | tf_op jit(solution)/shard_map/ppermute | solution.py:34
  78.8 2.0 %shard_map.90 = (bf16[256,640]{1,0:T(8,128)(2,1)S(1)}, bf16[256,640]{1,0:T(8,128)(2,1)S(1)}, bf16[256,640]{1,0:T(8,128)(2,1)S(1)}, bf16[256,640]{1,0:T(8,128)(2,1)S(1)}) custom-call(s32[5]{0:T(128)S(1)} %stack.83.coords.place, bf16[8,384,256]{2,1,0:T(8,128)(2,1)S(1)} %get-tuple-element.36.own, bf16[8,384,256]{2,1,0:T(8,128)(2,1)S(1)} %collective-permute-done.8.other, ...), custom_call_target="tpu_custom_call" | custom-call | flops 3019898880 | tf_op jit(solution)/shard_map/pallas_call | solution.py:144
  80.7 1.9 %collective-permute-done.17 = bf16[256,640]{1,0:T(8,128)(2,1)S(1)} collective-permute-done((bf16[256,640]{1,0:T(8,128)(2,1)S(1)}, bf16[256,640]{1,0:T(8,128)(2,1)S(1)}, u32[]{:S(2)}, u32[]{:S(2)}) %collective-permute-start.17) | collective-permute-done | bytes 327712 | tf_op jit(solution)/shard_map/ppermute | solution.py:34
  82.9 3.8 %collective-permute-start.18 = (bf16[2,256,640]{2,1,0:T(8,128)(2,1)S(1)}, bf16[2,256,640]{2,1,0:T(8,128)(2,1)S(1)}, u32[]{:S(2)}, u32[]{:S(2)}) collective-permute-start(bf16[2,256,640]{2,1,0:T(8,128)(2,1)S(1)} %pad_maximum_fusion.4), channel_id=1, source_target_pairs={{0,96},{1,97},{2,98},{3,99},{4,100},{5,101},{6,102},{7,103},{8,104... | collective-permute-start | bytes 1966088 | tf_op jit(solution)/shard_map/ppermute | solution.py:34
  86.9 4.9 %collective-permute-done.25 = bf16[2,384,512]{2,1,0:T(8,128)(2,1)S(1)} collective-permute-done((bf16[2,384,512]{2,1,0:T(8,128)(2,1)S(1)}, bf16[2,384,512]{2,1,0:T(8,128)(2,1)S(1)}, u32[]{:S(2)}, u32[]{:S(2)}) %collective-permute-start.25) | collective-permute-done | bytes 786464 | tf_op jit(solution)/shard_map/ppermute | solution.py:34
  96.1 4.0 %collective-permute-done.20 = bf16[4,256,384]{2,1,0:T(8,128)(2,1)S(1)} collective-permute-done((bf16[4,256,384]{2,1,0:T(8,128)(2,1)S(1)}, bf16[4,256,384]{2,1,0:T(8,128)(2,1)S(1)}, u32[]{:S(2)}, u32[]{:S(2)}) %collective-permute-start.20) | collective-permute-done | bytes 786464 | tf_op jit(solution)/shard_map/ppermute | solution.py:34
  100.4 3.2 %collective-permute-start.23 = (bf16[256,384]{1,0:T(8,128)(2,1)S(1)}, bf16[256,384]{1,0:T(8,128)(2,1)S(1)}, u32[]{:S(2)}, u32[]{:S(2)}) collective-permute-start(bf16[256,384]{1,0:T(8,128)(2,1)S(1)} %get-tuple-element.70), channel_id=1, source_target_pairs={{0,96},{1,97},{2,98},{3,99},{4,100},{5,101},{6,102},{7,103},{8,104... | collective-permute-start | bytes 589832 | tf_op jit(solution)/shard_map/ppermute | solution.py:34
  103.6 3.2 %collective-permute-done.16 = bf16[2,256,640]{2,1,0:T(8,128)(2,1)S(1)} collective-permute-done((bf16[2,256,640]{2,1,0:T(8,128)(2,1)S(1)}, bf16[2,256,640]{2,1,0:T(8,128)(2,1)S(1)}, u32[]{:S(2)}, u32[]{:S(2)}) %collective-permute-start.16) | collective-permute-done | bytes 655392 | tf_op jit(solution)/shard_map/ppermute | solution.py:34
  108.6 2.5 %collective-permute-done.21 = bf16[256,384]{1,0:T(8,128)(2,1)S(1)} collective-permute-done((bf16[256,384]{1,0:T(8,128)(2,1)S(1)}, bf16[256,384]{1,0:T(8,128)(2,1)S(1)}, u32[]{:S(2)}, u32[]{:S(2)}) %collective-permute-start.21) | collective-permute-done | bytes 196640 | tf_op jit(solution)/shard_map/ppermute | solution.py:34
  111.2 4.4 %collective-permute-done.19 = bf16[256,640]{1,0:T(8,128)(2,1)S(1)} collective-permute-done((bf16[256,640]{1,0:T(8,128)(2,1)S(1)}, bf16[256,640]{1,0:T(8,128)(2,1)S(1)}, u32[]{:S(2)}, u32[]{:S(2)}) %collective-permute-start.19) | collective-permute-done | bytes 327712 | tf_op jit(solution)/shard_map/ppermute | solution.py:34
  (84 shorter events, 31.8 us)
Async XLA Ops:
  0.6 12.4 %collective-permute-start.1 = (bf16[384,512]{1,0:T(8,128)(2,1)}, bf16[384,512]{1,0:T(8,128)(2,1)S(1)}, u32[]{:S(2)}, u32[]{:S(2)}) collective-permute-start(bf16[384,512]{1,0:T(8,128)(2,1)} %bitcast.92), channel_id=1, source_target_pairs={{0,1},{1,2},{2,3},{3,0},{4,5},{5,6},{6,7},{7,4},{8,9},{9,10},{10,1... | collective-permute-start | bytes 1179656 | tf_op jit(solution)/shard_map/ppermute | solution.py:34
  2.3 11.2 %collective-permute-start = (bf16[384,512]{1,0:T(8,128)(2,1)}, bf16[384,512]{1,0:T(8,128)(2,1)S(1)}, u32[]{:S(2)}, u32[]{:S(2)}) collective-permute-start(bf16[384,512]{1,0:T(8,128)(2,1)} %bitcast.93), channel_id=1, source_target_pairs={{0,3},{1,0},{2,1},{3,2},{4,7},{5,4},{6,5},{7,6},{8,11},{9,8},{10,9... | collective-permute-start | bytes 1179656 | tf_op jit(solution)/shard_map/ppermute | solution.py:34
  3.9 17.8 %collective-permute-start.4 = (bf16[384,512]{1,0:T(8,128)(2,1)}, bf16[384,512]{1,0:T(8,128)(2,1)S(1)}, u32[]{:S(2)}, u32[]{:S(2)}) collective-permute-start(bf16[384,512]{1,0:T(8,128)(2,1)} %bitcast.94), channel_id=1, source_target_pairs={{0,4},{1,5},{2,6},{3,7},{4,0},{5,1},{6,2},{7,3},{8,12},{9,13},{10,... | collective-permute-start | bytes 1179656 | tf_op jit(solution)/shard_map/ppermute | solution.py:34
  13.1 12.0 %collective-permute-start.2 = (bf16[192,512]{1,0:T(8,128)(2,1)S(1)}, bf16[192,512]{1,0:T(8,128)(2,1)S(1)}, u32[]{:S(2)}, u32[]{:S(2)}) collective-permute-start(bf16[192,512]{1,0:T(8,128)(2,1)S(1)} %slice.64), channel_id=1, source_target_pairs={{0,1},{1,2},{2,3},{3,0},{4,5},{5,6},{6,7},{7,4},{8,9},{9,10},{10,1... | collective-permute-start | bytes 589832 | tf_op jit(solution)/shard_map/ppermute | solution.py:34
  13.4 11.6 %collective-permute-start.3 = (bf16[192,512]{1,0:T(8,128)(2,1)S(1)}, bf16[192,512]{1,0:T(8,128)(2,1)S(1)}, u32[]{:S(2)}, u32[]{:S(2)}) collective-permute-start(bf16[192,512]{1,0:T(8,128)(2,1)S(1)} %slice.65), channel_id=1, source_target_pairs={{0,3},{1,0},{2,1},{3,2},{4,7},{5,4},{6,5},{7,6},{8,11},{9,8},{10,9... | collective-permute-start | bytes 589832 | tf_op jit(solution)/shard_map/ppermute | solution.py:34
  21.8 10.8 %collective-permute-start.7 = (bf16[384,512]{1,0:T(8,128)(2,1)S(1)}, bf16[384,512]{1,0:T(8,128)(2,1)S(1)}, u32[]{:S(2)}, u32[]{:S(2)}) collective-permute-start(bf16[384,512]{1,0:T(8,128)(2,1)S(1)} %collective-permute-done.4.refs_4_.refs_3_), channel_id=1, source_target_pairs={{0,1},{1,2},{2,3},{3,0},{4,5},{5,6},{6,7},{7,4},{8,9},{9,10},{10,1... | collective-permute-start | bytes 1179656 | tf_op jit(solution)/shard_map/ppermute | solution.py:34
  21.8 10.7 %collective-permute-start.5 = (bf16[384,512]{1,0:T(8,128)(2,1)S(1)}, bf16[384,512]{1,0:T(8,128)(2,1)S(1)}, u32[]{:S(2)}, u32[]{:S(2)}) collective-permute-start(bf16[384,512]{1,0:T(8,128)(2,1)S(1)} %collective-permute-done.4.refs_4_.refs_3_), channel_id=1, source_target_pairs={{0,3},{1,0},{2,1},{3,2},{4,7},{5,4},{6,5},{7,6},{8,11},{9,8},{10,9... | collective-permute-start | bytes 1179656 | tf_op jit(solution)/shard_map/ppermute | solution.py:34
  25.1 9.0 %collective-permute-start.6 = (bf16[384,512]{1,0:T(8,128)(2,1)S(1)}, bf16[384,512]{1,0:T(8,128)(2,1)S(1)}, u32[]{:S(2)}, u32[]{:S(2)}) collective-permute-start(bf16[384,512]{1,0:T(8,128)(2,1)S(1)} %constant_dynamic-update-slice_fusion.refs_2_.refs_4_), channel_id=1, source_target_pairs={{0,4},{1,5},{2,6},{3,7},{4,0},{5,1},{6,2},{7,3},{8,12},{9,13},{10,... | collective-permute-start | bytes 1179656 | tf_op jit(solution)/shard_map/ppermute | solution.py:34
  37.1 34.7 %collective-permute-start.8 = (bf16[8,384,256]{2,1,0:T(8,128)(2,1)S(1)}, bf16[8,384,256]{2,1,0:T(8,128)(2,1)S(1)}, u32[]{:S(2)}, u32[]{:S(2)}) collective-permute-start(bf16[8,384,256]{2,1,0:T(8,128)(2,1)S(1)} %get-tuple-element.37), channel_id=1, source_target_pairs={{0,8},{1,9},{2,10},{3,11},{4,12},{5,13},{6,14},{7,15},{8,0},{9,1},... | collective-permute-start | bytes 4718600 | tf_op jit(solution)/shard_map/ppermute | solution.py:34
  43.1 9.8 %collective-permute-start.13 = (f32[4,8,512]{2,1,0:T(8,128)S(1)}, f32[4,8,512]{2,1,0:T(8,128)S(1)}, u32[]{:S(2)}, u32[]{:S(2)}) collective-permute-start(f32[4,8,512]{2,1,0:T(8,128)S(1)} %pad_maximum_fusion.6), channel_id=1, source_target_pairs={{0,32},{1,33},{2,34},{3,35},{4,36},{5,37},{6,38},{7,39},{8,40},{9,... | collective-permute-start | bytes 196616 | tf_op jit(solution)/shard_map/ppermute | solution.py:34
  54.4 17.4 %collective-permute-start.14 = (bf16[384,1024]{1,0:T(8,128)(2,1)S(1)}, bf16[384,1024]{1,0:T(8,128)(2,1)S(1)}, u32[]{:S(2)}, u32[]{:S(2)}) collective-permute-start(bf16[384,1024]{1,0:T(8,128)(2,1)S(1)} %shard_map.88.d_own.deltas), channel_id=1, source_target_pairs={{0,8},{1,9},{2,10},{3,11},{4,12},{5,13},{6,14},{7,15},{8,0},{9,1},... | collective-permute-start | bytes 2359304 | tf_op jit(solution)/shard_map/ppermute | solution.py:34
  55.5 11.6 %collective-permute-start.26 = (bf16[384,512]{1,0:T(8,128)(2,1)S(1)}, bf16[384,512]{1,0:T(8,128)(2,1)S(1)}, u32[]{:S(2)}, u32[]{:S(2)}) collective-permute-start(bf16[384,512]{1,0:T(8,128)(2,1)S(1)} %get-tuple-element.67), channel_id=1, source_target_pairs={{0,3},{1,0},{2,1},{3,2},{4,7},{5,4},{6,5},{7,6},{8,11},{9,8},{10,9... | collective-permute-start | bytes 1179656 | tf_op jit(solution)/shard_map/ppermute | solution.py:34
  58.8 12.7 %collective-permute-start.24 = (bf16[384,512]{1,0:T(8,128)(2,1)S(1)}, bf16[384,512]{1,0:T(8,128)(2,1)S(1)}, u32[]{:S(2)}, u32[]{:S(2)}) collective-permute-start(bf16[384,512]{1,0:T(8,128)(2,1)S(1)} %get-tuple-element.63), channel_id=1, source_target_pairs={{0,1},{1,2},{2,3},{3,0},{4,5},{5,6},{6,7},{7,4},{8,9},{9,10},{10,1... | collective-permute-start | bytes 1179656 | tf_op jit(solution)/shard_map/ppermute | solution.py:34
  67.3 19.6 %collective-permute-start.27 = (bf16[2,384,512]{2,1,0:T(8,128)(2,1)S(1)}, bf16[2,384,512]{2,1,0:T(8,128)(2,1)S(1)}, u32[]{:S(2)}, u32[]{:S(2)}) collective-permute-start(bf16[2,384,512]{2,1,0:T(8,128)(2,1)S(1)} %pad_maximum_fusion.2), channel_id=1, source_target_pairs={{0,3},{1,0},{2,1},{3,2},{4,7},{5,4},{6,5},{7,6},{8,11},{9,8},{10,9... | collective-permute-start | bytes 2359304 | tf_op jit(solution)/shard_map/ppermute | solution.py:34
  71.7 20.1 %collective-permute-start.25 = (bf16[2,384,512]{2,1,0:T(8,128)(2,1)S(1)}, bf16[2,384,512]{2,1,0:T(8,128)(2,1)S(1)}, u32[]{:S(2)}, u32[]{:S(2)}) collective-permute-start(bf16[2,384,512]{2,1,0:T(8,128)(2,1)S(1)} %pad_maximum_fusion.1), channel_id=1, source_target_pairs={{0,1},{1,2},{2,3},{3,0},{4,5},{5,6},{6,7},{7,4},{8,9},{9,10},{10,1... | collective-permute-start | bytes 2359304 | tf_op jit(solution)/shard_map/ppermute | solution.py:34
  73.2 13.5 %collective-permute-start.15 = (bf16[256,640]{1,0:T(8,128)(2,1)S(1)}, bf16[256,640]{1,0:T(8,128)(2,1)S(1)}, u32[]{:S(2)}, u32[]{:S(2)}) collective-permute-start(bf16[256,640]{1,0:T(8,128)(2,1)S(1)} %get-tuple-element.47), channel_id=1, source_target_pairs={{0,32},{1,33},{2,34},{3,35},{4,36},{5,37},{6,38},{7,39},{8,40},{9,... | collective-permute-start | bytes 983048 | tf_op jit(solution)/shard_map/ppermute | solution.py:34
  73.4 9.3 %collective-permute-start.17 = (bf16[256,640]{1,0:T(8,128)(2,1)S(1)}, bf16[256,640]{1,0:T(8,128)(2,1)S(1)}, u32[]{:S(2)}, u32[]{:S(2)}) collective-permute-start(bf16[256,640]{1,0:T(8,128)(2,1)S(1)} %get-tuple-element.51), channel_id=1, source_target_pairs={{0,96},{1,97},{2,98},{3,99},{4,100},{5,101},{6,102},{7,103},{8,104... | collective-permute-start | bytes 983048 | tf_op jit(solution)/shard_map/ppermute | solution.py:34
  78.2 22.0 %collective-permute-start.20 = (bf16[4,256,384]{2,1,0:T(8,128)(2,1)S(1)}, bf16[4,256,384]{2,1,0:T(8,128)(2,1)S(1)}, u32[]{:S(2)}, u32[]{:S(2)}) collective-permute-start(bf16[4,256,384]{2,1,0:T(8,128)(2,1)S(1)} %pad_maximum_fusion), channel_id=1, source_target_pairs={{0,16},{1,17},{2,18},{3,19},{4,20},{5,21},{6,22},{7,23},{8,24},{9,... | collective-permute-start | bytes 2359304 | tf_op jit(solution)/shard_map/ppermute | solution.py:34
  82.9 20.8 %collective-permute-start.18 = (bf16[2,256,640]{2,1,0:T(8,128)(2,1)S(1)}, bf16[2,256,640]{2,1,0:T(8,128)(2,1)S(1)}, u32[]{:S(2)}, u32[]{:S(2)}) collective-permute-start(bf16[2,256,640]{2,1,0:T(8,128)(2,1)S(1)} %pad_maximum_fusion.4), channel_id=1, source_target_pairs={{0,96},{1,97},{2,98},{3,99},{4,100},{5,101},{6,102},{7,103},{8,104... | collective-permute-start | bytes 1966088 | tf_op jit(solution)/shard_map/ppermute | solution.py:34
  86.8 20.1 %collective-permute-start.16 = (bf16[2,256,640]{2,1,0:T(8,128)(2,1)S(1)}, bf16[2,256,640]{2,1,0:T(8,128)(2,1)S(1)}, u32[]{:S(2)}, u32[]{:S(2)}) collective-permute-start(bf16[2,256,640]{2,1,0:T(8,128)(2,1)S(1)} %pad_maximum_fusion.3), channel_id=1, source_target_pairs={{0,32},{1,33},{2,34},{3,35},{4,36},{5,37},{6,38},{7,39},{8,40},{9,... | collective-permute-start | bytes 1966088 | tf_op jit(solution)/shard_map/ppermute | solution.py:34
  91.9 15.7 %collective-permute-start.28 = (bf16[384,512]{1,0:T(8,128)(2,1)S(1)}, bf16[384,512]{1,0:T(8,128)(2,1)S(1)}, u32[]{:S(2)}, u32[]{:S(2)}) collective-permute-start(bf16[384,512]{1,0:T(8,128)(2,1)S(1)} %fusion), channel_id=1, source_target_pairs={{0,4},{1,5},{2,6},{3,7},{4,0},{5,1},{6,2},{7,3},{8,12},{9,13},{10,... | collective-permute-start | bytes 1179656 | tf_op jit(solution)/shard_map/ppermute | solution.py:34
  100.3 10.8 %collective-permute-start.21 = (bf16[256,384]{1,0:T(8,128)(2,1)S(1)}, bf16[256,384]{1,0:T(8,128)(2,1)S(1)}, u32[]{:S(2)}, u32[]{:S(2)}) collective-permute-start(bf16[256,384]{1,0:T(8,128)(2,1)S(1)} %get-tuple-element.69), channel_id=1, source_target_pairs={{0,32},{1,33},{2,34},{3,35},{4,36},{5,37},{6,38},{7,39},{8,40},{9,... | collective-permute-start | bytes 589832 | tf_op jit(solution)/shard_map/ppermute | solution.py:34
  100.4 10.7 %collective-permute-start.23 = (bf16[256,384]{1,0:T(8,128)(2,1)S(1)}, bf16[256,384]{1,0:T(8,128)(2,1)S(1)}, u32[]{:S(2)}, u32[]{:S(2)}) collective-permute-start(bf16[256,384]{1,0:T(8,128)(2,1)S(1)} %get-tuple-element.70), channel_id=1, source_target_pairs={{0,96},{1,97},{2,98},{3,99},{4,100},{5,101},{6,102},{7,103},{8,104... | collective-permute-start | bytes 589832 | tf_op jit(solution)/shard_map/ppermute | solution.py:34
  107.0 8.7 %collective-permute-start.19 = (bf16[256,640]{1,0:T(8,128)(2,1)S(1)}, bf16[256,640]{1,0:T(8,128)(2,1)S(1)}, u32[]{:S(2)}, u32[]{:S(2)}) collective-permute-start(bf16[256,640]{1,0:T(8,128)(2,1)S(1)} %fusion.3), channel_id=1, source_target_pairs={{0,16},{1,17},{2,18},{3,19},{4,20},{5,21},{6,22},{7,23},{8,24},{9,... | collective-permute-start | bytes 983048 | tf_op jit(solution)/shard_map/ppermute | solution.py:34
  (7 other events, 44.2 us)
